TPU v7x, 32 devices: a whole 2x2x4 slice. The times are simulated.
32 devices in a mesh: section: 2 (over core), ctx: 8 (over z, x), dp: 2 (over y).
Axes of the slice: x: 2, y: 2, z: 4, core: 2. Of those that a mesh axis runs over, the one named last changes fastest.
Arguments:
- hidden: bfloat16 [4, 2048, 5376], P(('section', 'dp'), 'ctx'), may hold values from -6 to 6
- frozen_query_rows: bfloat16 [4, 2048, 2048], P(('section', 'dp'), 'ctx'), may hold values from -12 to 12
- frozen_key_rows: bfloat16 [4, 2048, 1024], P(('section', 'dp'), 'ctx'), may hold values from -12 to 12
- frozen_value_rows: bfloat16 [4, 2048, 1024], P(('section', 'dp'), 'ctx'), may hold values from -6 to 6
- next_output_gradient: bfloat16 [4, 2048, 2048], P(('section', 'dp'), 'ctx'), may hold values from -0.011962891 to 0.011962891
- document_lengths: int32 [4, 16], P(('section', 'dp')), may hold values from 1 to 512, 2048 in all within a row
- document_adapter: int32 [4, 16], P(('section', 'dp')), may hold values from 0 to 3
- adapter_down_maps: bfloat16 [5376, 2, 4, 16], replicated, may hold values from -0.078125 to 0.078125
- adapter_up_maps: bfloat16 [2, 4, 16, 1024], replicated, may hold values from -1.5 to 1.5
Outputs:
- handed_on: bfloat16 [4, 2048, 2048], P(('section', 'dp'), 'ctx')
- down_map_gradient: float32 [5376, 2, 4, 16], replicated
- up_map_gradient: float32 [2, 4, 16, 1024], replicated
Inputs may be any that keep to these rules, and one draw needn't show every extreme that they name: `document_lengths`: each sequence's 16 lengths sum to 2048, and the longest is exactly 512.
All inputs are finite; a program needn't handle non-finite values.
Results may differ from a plain program's by a relative error of at most 0.016.
Values may be sent and summed in bfloat16 or wider, within the bound.
No kernel may reach another device: no remote copies, remote signals or barrier semaphores. Data moves between devices by JAX's collectives and lax.ppermute only.
A program may use at most 128 MiB of HBM per device.

v0:
```python
from functools import partial
import jax
import jax.numpy as jnp
from jax import lax
from jax.sharding import PartitionSpec as P

HD = 128
WINDOW = 1024
query_scale = 168.0 ** (-0.5)
adapter_scale = 0.5
rope_base = 10000.0
masked_score = -1e30


def passed_along(value, axis, by):
    length = lax.axis_size(axis)
    return lax.ppermute(value, axis, [(i, (i + by) % length) for i in range(length)])


def passed_along_2(value, axis, steps):
    count = lax.axis_size(axis)
    initial, last = (max(0, -steps), min(count, count - steps))
    return lax.ppermute(value, axis, [(source, source + steps) for source in range(initial, last)])


def rotate(vectors, positions, direction):
    head_dim = vectors.shape[-1]
    half_dim = head_dim // 2
    frequency = rope_base ** (-(jnp.arange(half_dim, dtype=jnp.float32) * 2.0) / head_dim)
    angles = positions[:, None] * frequency[None, :]
    cos_part = jnp.cos(angles)[:, None, :]
    sine_part = direction * jnp.sin(angles)[:, None, :]
    front_half = vectors[..., :half_dim]
    back_half = vectors[..., half_dim:]
    return jnp.concatenate(
        [
            front_half * cos_part - back_half * sine_part,
            back_half * cos_part + front_half * sine_part,
        ],
        axis=-1,
    )


def doc_index(sequence_lengths, positions):
    doc_ends = jnp.cumsum(sequence_lengths)
    return jnp.sum((doc_ends[None, :] <= positions[:, None]).astype(jnp.int32), axis=1)


def tenant_rows(sequence_lengths, adapter_bank, positions):
    doc_ids = doc_index(sequence_lengths, positions)
    picked = (
        doc_ids[:, None] == jnp.arange(sequence_lengths.shape[0], dtype=jnp.int32)[None, :]
    ).astype(jnp.int32)
    return (doc_ids, jnp.sum(picked * adapter_bank[None, :], axis=1))


def adapter_token_rows(
    hidden, frozen_key_rows, frozen_value_rows, adapter_down_maps, adapter_up_maps, adapter_choice
):
    token_row_count = hidden.shape[0]
    adapter_choices = adapter_up_maps.shape[1]
    adapter_rank_size = adapter_up_maps.shape[2]
    key_value_width = adapter_up_maps.shape[3]
    adapter_onehot_mask = (
        adapter_choice[:, None] == jnp.arange(adapter_choices, dtype=jnp.int32)[None, :]
    ).astype(jnp.float32)
    low_rank_rows = jnp.dot(
        hidden,
        adapter_down_maps.reshape(
            adapter_down_maps.shape[0], 2 * adapter_choices * adapter_rank_size
        ),
        preferred_element_type=jnp.float32,
    )
    low_rank_rows = low_rank_rows.reshape(token_row_count, 2, adapter_choices, adapter_rank_size)
    low_rank = jnp.sum(low_rank_rows * adapter_onehot_mask[:, None, :, None], axis=2).astype(
        jnp.bfloat16
    )
    adapter_spread = low_rank[:, :, None, :] * adapter_onehot_mask[:, None, :, None].astype(
        jnp.bfloat16
    )
    key_adapter_shift = jnp.dot(
        adapter_spread[:, 0].reshape(token_row_count, adapter_choices * adapter_rank_size),
        adapter_up_maps[0].reshape(adapter_choices * adapter_rank_size, key_value_width),
        preferred_element_type=jnp.float32,
    )
    value_adapter_shift = jnp.dot(
        adapter_spread[:, 1].reshape(token_row_count, adapter_choices * adapter_rank_size),
        adapter_up_maps[1].reshape(adapter_choices * adapter_rank_size, key_value_width),
        preferred_element_type=jnp.float32,
    )
    key_before_rotary = frozen_key_rows.astype(jnp.float32) + adapter_scale * key_adapter_shift
    value_token_rows = (
        frozen_value_rows.astype(jnp.float32) + adapter_scale * value_adapter_shift
    ).astype(jnp.bfloat16)
    return (adapter_onehot_mask, adapter_spread, key_before_rotary, value_token_rows)


def adapter_gradients(
    hidden, adapter_spread, adapter_onehot_mask, key_gradient, value_gradient, adapter_up_maps
):
    token_row_count = hidden.shape[0]
    adapter_choices = adapter_up_maps.shape[1]
    adapter_rank_size = adapter_up_maps.shape[2]
    key_value_width = adapter_up_maps.shape[3]
    up_gradient_parts = []
    down_parts = []
    for adapter_selector, adapter_field_gradient in ((0, key_gradient), (1, value_gradient)):
        flat_adapter_spread = adapter_spread[:, adapter_selector].reshape(
            token_row_count, adapter_choices * adapter_rank_size
        )
        up_gradient_parts.append(
            adapter_scale
            * jnp.dot(
                flat_adapter_spread.T, adapter_field_gradient, preferred_element_type=jnp.float32
            )
        )
        low_rank_gradient = adapter_scale * jnp.dot(
            adapter_field_gradient,
            adapter_up_maps[adapter_selector]
            .reshape(adapter_choices * adapter_rank_size, key_value_width)
            .T,
            preferred_element_type=jnp.float32,
        )
        down_parts.append(
            (
                low_rank_gradient.reshape(token_row_count, adapter_choices, adapter_rank_size)
                * adapter_onehot_mask[:, :, None]
            ).astype(jnp.bfloat16)
        )
    up_map_gradient = jnp.stack(up_gradient_parts).reshape(
        2, adapter_choices, adapter_rank_size, key_value_width
    )
    low_grads = jnp.stack(down_parts, axis=1).reshape(
        token_row_count, 2 * adapter_choices * adapter_rank_size
    )
    down_map_gradient = jnp.dot(hidden.T, low_grads, preferred_element_type=jnp.float32).reshape(
        hidden.shape[1], 2, adapter_choices, adapter_rank_size
    )
    return (down_map_gradient, up_map_gradient)


def masked_scores(query_part, key_part, allowed):
    scores = (
        jnp.einsum("trd,ld->trl", query_part, key_part, preferred_element_type=jnp.float32)
        * query_scale
    )
    return jnp.where(allowed[:, None, :], scores, masked_score)


def group_forward(operands, allowed):
    query_part, key_part, value_part = operands
    scores = masked_scores(query_part, key_part, allowed)
    row_max = jnp.max(scores, axis=2, keepdims=True)
    shifted = jnp.exp(scores - row_max)
    row_total = jnp.sum(shifted, axis=2, keepdims=True)
    weights = (shifted / row_total).astype(jnp.bfloat16)
    output_rows = jnp.einsum(
        "trl,ld->trd", weights, value_part, preferred_element_type=jnp.float32
    ).astype(jnp.bfloat16)
    return (output_rows, (row_max + jnp.log(row_total))[..., 0])


def group_backward(operands, allowed):
    query_part, key_part, value_part, out_part, grad_part, log_total = operands
    scores = masked_scores(query_part, key_part, allowed)
    weights = jnp.exp(scores - log_total[:, :, None])
    weights_low = weights.astype(jnp.bfloat16)
    drift_rows = jnp.sum(grad_part.astype(jnp.float32) * out_part.astype(jnp.float32), axis=2)
    grad_weights = jnp.einsum(
        "trd,ld->trl", grad_part, value_part, preferred_element_type=jnp.float32
    )
    grad_scores = (weights * (grad_weights - drift_rows[:, :, None])).astype(jnp.bfloat16)
    value_step = jnp.einsum(
        "trl,trd->ld", weights_low, grad_part, preferred_element_type=jnp.float32
    )
    key_step = (
        jnp.einsum("trl,trd->ld", grad_scores, query_part, preferred_element_type=jnp.float32)
        * query_scale
    )
    return (key_step, value_step)


def body(
    hidden,
    frozen_query_rows,
    frozen_key_rows,
    frozen_value_rows,
    next_output_gradient,
    document_lengths,
    document_adapter,
    adapter_down_maps,
    adapter_up_maps,
):
    tok_rows = hidden.shape[1]
    query_width = frozen_query_rows.shape[2]
    key_value_width = frozen_key_rows.shape[2]
    kv_heads = key_value_width // HD
    group_size = query_width // key_value_width
    ctx_index = lax.axis_index("ctx")
    reach_devs = min(WINDOW // tok_rows, lax.axis_size("ctx") - 1)
    returned_values = passed_along(next_output_gradient, "section", -1)
    positions = ctx_index * tok_rows + jnp.arange(tok_rows, dtype=jnp.int32)
    doc_ids, adapter_choice = tenant_rows(document_lengths[0], document_adapter[0], positions)
    adapter_onehot_mask, adapter_spread, key_before_rotary, value_token_rows = adapter_token_rows(
        hidden[0],
        frozen_key_rows[0],
        frozen_value_rows[0],
        adapter_down_maps,
        adapter_up_maps,
        adapter_choice,
    )
    pos_float = positions.astype(jnp.float32)
    key_rows = (
        rotate(key_before_rotary.reshape(tok_rows, kv_heads, HD), pos_float, 1.0)
        .astype(jnp.bfloat16)
        .reshape(tok_rows, key_value_width)
    )
    query_rows = rotate(
        frozen_query_rows[0].astype(jnp.float32).reshape(tok_rows, kv_heads * group_size, HD),
        pos_float,
        1.0,
    ).astype(jnp.bfloat16)
    received = []
    moving = (key_rows, value_token_rows)
    for distance in range(reach_devs):
        moving = passed_along_2((moving[0], moving[1]), "ctx", 1)
        received.append(moving)
    far_first = received[::-1]
    key_all = jnp.concatenate([kv_pair[0] for kv_pair in far_first] + [key_rows], axis=0)
    value_all = jnp.concatenate([kv_pair[1] for kv_pair in far_first] + [value_token_rows], axis=0)
    key_pos = (ctx_index - reach_devs) * tok_rows + jnp.arange(
        (reach_devs + 1) * tok_rows, dtype=jnp.int32
    )
    key_docs = doc_index(document_lengths[0], key_pos)
    key_gap = positions[:, None] - key_pos[None, :]
    allowed = (
        (doc_ids[:, None] == key_docs[None, :])
        & (key_gap >= 0)
        & (key_gap < WINDOW)
        & (key_pos >= 0)[None, :]
    )
    query_groups = jnp.moveaxis(query_rows.reshape(tok_rows, kv_heads, group_size, HD), 1, 0)
    key_groups = jnp.moveaxis(key_all.reshape(-1, kv_heads, HD), 1, 0)
    value_groups = jnp.moveaxis(value_all.reshape(-1, kv_heads, HD), 1, 0)
    out_groups, log_groups = lax.map(
        partial(group_forward, allowed=allowed), (query_groups, key_groups, value_groups)
    )
    attention_output = jnp.moveaxis(out_groups, 0, 1).reshape(1, tok_rows, query_width)
    handed = passed_along(attention_output, "section", 1)
    grad_groups = jnp.moveaxis(returned_values[0].reshape(tok_rows, kv_heads, group_size, HD), 1, 0)
    key_grads, value_grads = lax.map(
        partial(group_backward, allowed=allowed),
        (query_groups, key_groups, value_groups, out_groups, grad_groups, log_groups),
    )
    key_grads = jnp.moveaxis(key_grads, 0, 1).reshape(-1, key_value_width)
    value_grads = jnp.moveaxis(value_grads, 0, 1).reshape(-1, key_value_width)

    def rows_at(field_rows, distance):
        return field_rows[
            (reach_devs - distance) * tok_rows : (reach_devs - distance + 1) * tok_rows
        ]

    carried = (rows_at(key_grads, reach_devs), rows_at(value_grads, reach_devs))
    for distance in range(reach_devs - 1, -1, -1):
        carried = passed_along_2((carried[0], carried[1]), "ctx", -1)
        carried = (
            carried[0] + rows_at(key_grads, distance),
            carried[1] + rows_at(value_grads, distance),
        )
    key_back, value_back = carried
    key_gradient = (
        rotate(key_back.reshape(tok_rows, kv_heads, HD), pos_float, -1.0)
        .astype(jnp.bfloat16)
        .reshape(tok_rows, key_value_width)
    )
    value_gradient = value_back.astype(jnp.bfloat16)
    down_map_gradient, up_map_gradient = adapter_gradients(
        hidden[0],
        adapter_spread,
        adapter_onehot_mask,
        key_gradient,
        value_gradient,
        adapter_up_maps,
    )
    summed = lax.psum((down_map_gradient, up_map_gradient), ("section", "ctx", "dp"))
    return (handed, summed[0], summed[1])


def solution(mesh):
    return jax.shard_map(
        body,
        mesh=mesh,
        in_specs=(
            P(("section", "dp"), "ctx", None),
            P(("section", "dp"), "ctx", None),
            P(("section", "dp"), "ctx", None),
            P(("section", "dp"), "ctx", None),
            P(("section", "dp"), "ctx", None),
            P(("section", "dp"), None),
            P(("section", "dp"), None),
            P(),
            P(),
        ),
        out_specs=(P(("section", "dp"), "ctx", None), P(), P()),
        check_vma=False,
    )
```

profile of v0, /device:TPU:0, one launch (start us, length us, event | category | flops | bytes accessed | tf_op | source)
XLA Modules:
  0.0 638.7 jit_solution(13565225289575519029)
XLA Ops:
  17.9 5.7 collective-permute-start
  28.1 6.9 %collective-permute-done = bf16[256,1024]{0,1:T(8,128)(2,1)} collective-permute-done((bf16[256,1024]{0,1:T(8,128)(2,1)S(1)}, bf16[256,1024]{0,1:T(8,128)(2,1)}, u32[]{:S(2)}, u32[]{:S(2)}) %collective-permute-start) | collective-permute-done | bytes 524320 | tf_op jit(solution)/shard_map/ppermute | solution.py:23
  35.0 5.3 collective-permute-start.1
  46.4 5.2 collective-permute-start.5
  51.5 6.1 collective-permute-done.1
  57.6 5.2 collective-permute-start.2
  68.8 5.2 collective-permute-start.6
  74.0 6.0 collective-permute-done.2
  80.1 4.4 collective-permute-start.3
  91.3 5.2 collective-permute-start.7
  96.5 6.1 collective-permute-done.3
  109.8 4.4 copy.48
  121.6 46.0 %while.26 = (s32[]{:T(128)}, bf16[8,256,2,128]{3,1,2,0:T(8,128)(2,1)}, f32[8,256,2]{1,2,0:T(2,128)}, bf16[8,256,2,128]{3,1,2,0:T(8,128)(2,1)}, bf16[8,1280,128]{...) while((s32[]{:T(128)}, ...), condition=%wide.region_8.9_spmd.clone, body=%wide.region_5.8_spmd.clone.sunk | while | flops 343145984 | bytes 9469813 | solution.py:245
  167.7 127.0 %while.27 = (s32[]{:T(128)}, f32[8,1280,128]{1,2,0:T(8,128)}, f32[8,1280,128]{1,2,0:T(8,128)}, bf16[8,256,2,128]{3,1,2,0:T(8,128)(2,1)}, bf16[8,1280,128]{2,1,0:...) while((s32[]{:T(128)}, f32[8,1280,128]{1,2,0:T(8,128)}, ...), condition=%wide.region_11.12_spmd.clone, body=%wide.region_9.11_spmd.clone.sunk | while | flops 678395392 | bytes 14472769 | solution.py:251
  253.8 3.9 fusion.130
  301.2 24.9 %collective-permute-done.14 = f32[256,1024]{0,1:T(8,128)S(1)} collective-permute-done((f32[256,1024]{0,1:T(8,128)S(1)}, f32[256,1024]{0,1:T(8,128)S(1)}, u32[]{:S(2)}, u32[]{:S(2)}) %collective-permute-start.14) | collective-permute-done | bytes 1048608 | tf_op jit(solution)/shard_map/ppermute | solution.py:23
  327.6 21.0 %collective-permute-done.10 = f32[256,1024]{0,1:T(8,128)S(1)} collective-permute-done((f32[256,1024]{0,1:T(8,128)S(1)}, f32[256,1024]{0,1:T(8,128)S(1)}, u32[]{:S(2)}, u32[]{:S(2)}) %collective-permute-start.10) | collective-permute-done | bytes 1048608 | tf_op jit(solution)/shard_map/ppermute | solution.py:23
  350.1 21.0 %collective-permute-done.15 = f32[256,1024]{0,1:T(8,128)S(1)} collective-permute-done((f32[256,1024]{0,1:T(8,128)S(1)}, f32[256,1024]{0,1:T(8,128)S(1)}, u32[]{:S(2)}, u32[]{:S(2)}) %collective-permute-start.15) | collective-permute-done | bytes 1048608 | tf_op jit(solution)/shard_map/ppermute | solution.py:23
  372.6 21.0 %collective-permute-done.11 = f32[256,1024]{0,1:T(8,128)S(1)} collective-permute-done((f32[256,1024]{0,1:T(8,128)S(1)}, f32[256,1024]{0,1:T(8,128)S(1)}, u32[]{:S(2)}, u32[]{:S(2)}) %collective-permute-start.11) | collective-permute-done | bytes 1048608 | tf_op jit(solution)/shard_map/ppermute | solution.py:23
  395.0 21.0 %collective-permute-done.16 = f32[256,1024]{0,1:T(8,128)S(1)} collective-permute-done((f32[256,1024]{0,1:T(8,128)S(1)}, f32[256,1024]{0,1:T(8,128)S(1)}, u32[]{:S(2)}, u32[]{:S(2)}) %collective-permute-start.16) | collective-permute-done | bytes 1048608 | tf_op jit(solution)/shard_map/ppermute | solution.py:23
  417.5 21.0 %collective-permute-done.12 = f32[256,1024]{0,1:T(8,128)S(1)} collective-permute-done((f32[256,1024]{0,1:T(8,128)S(1)}, f32[256,1024]{0,1:T(8,128)S(1)}, u32[]{:S(2)}, u32[]{:S(2)}) %collective-permute-start.12) | collective-permute-done | bytes 1048608 | tf_op jit(solution)/shard_map/ppermute | solution.py:23
  440.3 20.8 %collective-permute-done.17 = f32[256,1024]{0,1:T(8,128)S(1)} collective-permute-done((f32[256,1024]{0,1:T(8,128)S(1)}, f32[256,1024]{0,1:T(8,128)S(1)}, u32[]{:S(2)}, u32[]{:S(2)}) %collective-permute-start.17) | collective-permute-done | bytes 1048608 | tf_op jit(solution)/shard_map/ppermute | solution.py:23
  461.7 18.9 %collective-permute-done.13 = f32[256,1024]{0,1:T(8,128)S(1)} collective-permute-done((f32[256,1024]{0,1:T(8,128)S(1)}, f32[256,1024]{0,1:T(8,128)S(1)}, u32[]{:S(2)}, u32[]{:S(2)}) %collective-permute-start.13) | collective-permute-done | bytes 1048608 | tf_op jit(solution)/shard_map/ppermute | solution.py:23
  493.7 131.4 %all-reduce.3.cloned.1.call-done = (f32[5376,2,4,16]{0,3,2,1:T(8,128)}, f32[2,4,16,1024]{3,2,1,0:T(8,128)}) async-done(((f32[5376,2,4,16]{0,3,2,1:T(8,128)}, f32[2,4,16,1024]{3,2,1,0:T(8,128)}), (f32[5376,2,4,16]{0,3,2,1:T(8,128)}, f32[2,4,16,1024]{3,2,1,0:T(8,128)})) %all-reduce.3.cloned.1.call-update) | async-done | bytes 3276816 | tf_op jit(solution)/shard_map/psum | solution.py:285
  (343 shorter events, 252.8 us)
Async XLA Ops:
  7.2 618.0 %all-reduce.3.cloned.1.call-start = ((), (), s32[]{:S(2)}) async-start(), calls=%async_computation | async-start | bytes 6553600 | tf_op jit(solution)/shard_map/psum | solution.py:285
  15.5 8.0 %copy-start.22 = (bf16[1,256,1024]{2,1,0:T(8,128)(2,1)S(1)}, bf16[1,256,1024]{2,1,0:T(8,128)(2,1)}, u32[]{:S(2)}) copy-start(bf16[1,256,1024]{2,1,0:T(8,128)(2,1)} %param.16) | copy-start | bytes 1572868
  17.9 17.2 %collective-permute-start = (bf16[256,1024]{0,1:T(8,128)(2,1)S(1)}, bf16[256,1024]{0,1:T(8,128)(2,1)}, u32[]{:S(2)}, u32[]{:S(2)}) collective-permute-start(bf16[256,1024]{0,1:T(8,128)(2,1)S(1)} %bitcast.243), channel_id=1, source_target_pairs={{0,2},{2,4},{4,6},{6,8},{8,10},{10,12},{12,14},{1,3},{3,5},{5,7},{... | collective-permute-start | bytes 1572872 | tf_op jit(solution)/shard_map/ppermute | solution.py:23
  24.7 21.7 %collective-permute-start.4 = (bf16[256,1024]{1,0:T(8,128)(2,1)}, bf16[256,1024]{1,0:T(8,128)(2,1)}, u32[]{:S(2)}, u32[]{:S(2)}) collective-permute-start(bf16[256,1024]{1,0:T(8,128)(2,1)} %fusion.59), channel_id=1, source_target_pairs={{0,2},{2,4},{4,6},{6,8},{8,10},{10,12},{12,14},{1,3},{3,5},{5,7},{... | collective-permute-start | bytes 1572872 | tf_op jit(solution)/shard_map/ppermute | solution.py:23
  35.0 22.6 %collective-permute-start.1 = (bf16[256,1024]{0,1:T(8,128)(2,1)}, bf16[256,1024]{0,1:T(8,128)(2,1)}, u32[]{:S(2)}, u32[]{:S(2)}) collective-permute-start(bf16[256,1024]{0,1:T(8,128)(2,1)} %collective-permute-done), channel_id=1, source_target_pairs={{0,2},{2,4},{4,6},{6,8},{8,10},{10,12},{12,14},{1,3},{3,5},{5,7},{... | collective-permute-start | bytes 1572872 | tf_op jit(solution)/shard_map/ppermute | solution.py:23
  42.6 125.1 %collective-permute-start.9 = (bf16[1,256,2048]{1,2,0:T(8,128)(2,1)}, bf16[1,256,2048]{1,2,0:T(8,128)(2,1)}, u32[]{:S(2)}, u32[]{:S(2)}) collective-permute-start(bf16[1,256,2048]{1,2,0:T(8,128)(2,1)} %copy.50), channel_id=1, source_target_pairs={{0,16},{16,0},{1,17},{17,1},{2,18},{18,2},{3,19},{19,3},{4,20},{20... | collective-permute-start | bytes 3145736 | tf_op jit(solution)/shard_map/ppermute | solution.py:17
  46.4 22.5 %collective-permute-start.5 = (bf16[256,1024]{1,0:T(8,128)(2,1)}, bf16[256,1024]{1,0:T(8,128)(2,1)}, u32[]{:S(2)}, u32[]{:S(2)}) collective-permute-start(bf16[256,1024]{1,0:T(8,128)(2,1)} %collective-permute-done.4), channel_id=1, source_target_pairs={{0,2},{2,4},{4,6},{6,8},{8,10},{10,12},{12,14},{1,3},{3,5},{5,7},{... | collective-permute-start | bytes 1572872 | tf_op jit(solution)/shard_map/ppermute | solution.py:23
  57.6 22.5 %collective-permute-start.2 = (bf16[256,1024]{0,1:T(8,128)(2,1)}, bf16[256,1024]{0,1:T(8,128)(2,1)}, u32[]{:S(2)}, u32[]{:S(2)}) collective-permute-start(bf16[256,1024]{0,1:T(8,128)(2,1)} %collective-permute-done.1), channel_id=1, source_target_pairs={{0,2},{2,4},{4,6},{6,8},{8,10},{10,12},{12,14},{1,3},{3,5},{5,7},{... | collective-permute-start | bytes 1572872 | tf_op jit(solution)/shard_map/ppermute | solution.py:23
  66.9 17.6 %copy-start.1 = (f32[256,64]{1,0:T(8,128)S(1)}, f32[256,64]{1,0:T(8,128)}, u32[]{:S(2)}) copy-start(f32[256,64]{1,0:T(8,128)} %copy.41) | copy-start | bytes 196612
  66.9 17.6 %copy-start.2 = (f32[256,64]{1,0:T(8,128)S(1)}, f32[256,64]{1,0:T(8,128)}, u32[]{:S(2)}) copy-start(f32[256,64]{1,0:T(8,128)} %copy.43) | copy-start | bytes 196612
  68.8 22.5 %collective-permute-start.6 = (bf16[256,1024]{1,0:T(8,128)(2,1)}, bf16[256,1024]{1,0:T(8,128)(2,1)}, u32[]{:S(2)}, u32[]{:S(2)}) collective-permute-start(bf16[256,1024]{1,0:T(8,128)(2,1)} %collective-permute-done.5), channel_id=1, source_target_pairs={{0,2},{2,4},{4,6},{6,8},{8,10},{10,12},{12,14},{1,3},{3,5},{5,7},{... | collective-permute-start | bytes 1572872 | tf_op jit(solution)/shard_map/ppermute | solution.py:23
  80.1 22.5 %collective-permute-start.3 = (bf16[256,1024]{0,1:T(8,128)(2,1)}, bf16[256,1024]{0,1:T(8,128)(2,1)S(1)}, u32[]{:S(2)}, u32[]{:S(2)}) collective-permute-start(bf16[256,1024]{0,1:T(8,128)(2,1)} %collective-permute-done.2), channel_id=1, source_target_pairs={{0,2},{2,4},{4,6},{6,8},{8,10},{10,12},{12,14},{1,3},{3,5},{5,7},{... | collective-permute-start | bytes 1572872 | tf_op jit(solution)/shard_map/ppermute | solution.py:23
  91.3 22.9 %collective-permute-start.7 = (bf16[256,1024]{1,0:T(8,128)(2,1)}, bf16[256,1024]{1,0:T(8,128)(2,1)}, u32[]{:S(2)}, u32[]{:S(2)}) collective-permute-start(bf16[256,1024]{1,0:T(8,128)(2,1)} %collective-permute-done.6), channel_id=1, source_target_pairs={{0,2},{2,4},{4,6},{6,8},{8,10},{10,12},{12,14},{1,3},{3,5},{5,7},{... | collective-permute-start | bytes 1572872 | tf_op jit(solution)/shard_map/ppermute | solution.py:23
  297.8 28.4 %collective-permute-start.14 = (f32[256,1024]{0,1:T(8,128)S(1)}, f32[256,1024]{0,1:T(8,128)S(1)}, u32[]{:S(2)}, u32[]{:S(2)}) collective-permute-start(f32[256,1024]{0,1:T(8,128)S(1)} %bitcast.238), channel_id=1, source_target_pairs={{2,0},{4,2},{6,4},{8,6},{10,8},{12,10},{14,12},{3,1},{5,3},{7,5},{... | collective-permute-start | bytes 3145736 | tf_op jit(solution)/shard_map/ppermute | solution.py:23
  299.9 48.7 %collective-permute-start.10 = (f32[256,1024]{0,1:T(8,128)S(1)}, f32[256,1024]{0,1:T(8,128)S(1)}, u32[]{:S(2)}, u32[]{:S(2)}) collective-permute-start(f32[256,1024]{0,1:T(8,128)S(1)} %bitcast.239), channel_id=1, source_target_pairs={{2,0},{4,2},{6,4},{8,6},{10,8},{12,10},{14,12},{3,1},{5,3},{7,5},{... | collective-permute-start | bytes 3145736 | tf_op jit(solution)/shard_map/ppermute | solution.py:23
  326.3 44.8 %collective-permute-start.15 = (f32[256,1024]{0,1:T(8,128)S(1)}, f32[256,1024]{0,1:T(8,128)S(1)}, u32[]{:S(2)}, u32[]{:S(2)}) collective-permute-start(f32[256,1024]{0,1:T(8,128)S(1)} %bitcast_add_fusion.3), channel_id=1, source_target_pairs={{2,0},{4,2},{6,4},{8,6},{10,8},{12,10},{14,12},{3,1},{5,3},{7,5},{... | collective-permute-start | bytes 3145736 | tf_op jit(solution)/shard_map/ppermute | solution.py:23
  348.8 44.8 %collective-permute-start.11 = (f32[256,1024]{0,1:T(8,128)S(1)}, f32[256,1024]{0,1:T(8,128)S(1)}, u32[]{:S(2)}, u32[]{:S(2)}) collective-permute-start(f32[256,1024]{0,1:T(8,128)S(1)} %bitcast_add_fusion.7), channel_id=1, source_target_pairs={{2,0},{4,2},{6,4},{8,6},{10,8},{12,10},{14,12},{3,1},{5,3},{7,5},{... | collective-permute-start | bytes 3145736 | tf_op jit(solution)/shard_map/ppermute | solution.py:23
  371.3 44.8 %collective-permute-start.16 = (f32[256,1024]{0,1:T(8,128)S(1)}, f32[256,1024]{0,1:T(8,128)S(1)}, u32[]{:S(2)}, u32[]{:S(2)}) collective-permute-start(f32[256,1024]{0,1:T(8,128)S(1)} %bitcast_add_fusion.2), channel_id=1, source_target_pairs={{2,0},{4,2},{6,4},{8,6},{10,8},{12,10},{14,12},{3,1},{5,3},{7,5},{... | collective-permute-start | bytes 3145736 | tf_op jit(solution)/shard_map/ppermute | solution.py:23
  393.7 44.8 %collective-permute-start.12 = (f32[256,1024]{0,1:T(8,128)S(1)}, f32[256,1024]{0,1:T(8,128)S(1)}, u32[]{:S(2)}, u32[]{:S(2)}) collective-permute-start(f32[256,1024]{0,1:T(8,128)S(1)} %bitcast_add_fusion.6), channel_id=1, source_target_pairs={{2,0},{4,2},{6,4},{8,6},{10,8},{12,10},{14,12},{3,1},{5,3},{7,5},{... | collective-permute-start | bytes 3145736 | tf_op jit(solution)/shard_map/ppermute | solution.py:23
  416.1 24.1 %copy-start.6 = (bf16[2,4,16,1024]{3,2,1,0:T(8,128)(2,1)S(1)}, bf16[2,4,16,1024]{3,2,1,0:T(8,128)(2,1)}, u32[]{:S(2)}) copy-start(bf16[2,4,16,1024]{3,2,1,0:T(8,128)(2,1)} %param.21) | copy-start | bytes 786436
  416.2 44.8 %collective-permute-start.17 = (f32[256,1024]{0,1:T(8,128)S(1)}, f32[256,1024]{0,1:T(8,128)S(1)}, u32[]{:S(2)}, u32[]{:S(2)}) collective-permute-start(f32[256,1024]{0,1:T(8,128)S(1)} %bitcast_add_fusion.1), channel_id=1, source_target_pairs={{2,0},{4,2},{6,4},{8,6},{10,8},{12,10},{14,12},{3,1},{5,3},{7,5},{... | collective-permute-start | bytes 3145736 | tf_op jit(solution)/shard_map/ppermute | solution.py:23
  438.7 42.0 %collective-permute-start.13 = (f32[256,1024]{0,1:T(8,128)S(1)}, f32[256,1024]{0,1:T(8,128)S(1)}, u32[]{:S(2)}, u32[]{:S(2)}) collective-permute-start(f32[256,1024]{0,1:T(8,128)S(1)} %bitcast_add_fusion.5), channel_id=1, source_target_pairs={{2,0},{4,2},{6,4},{8,6},{10,8},{12,10},{14,12},{3,1},{5,3},{7,5},{... | collective-permute-start | bytes 3145736 | tf_op jit(solution)/shard_map/ppermute | solution.py:23
  461.2 19.6 %copy-start.7 = (f32[256,64]{0,1:T(8,128)S(1)}, f32[256,64]{0,1:T(8,128)}, u32[]{:S(2)}) copy-start(f32[256,64]{0,1:T(8,128)} %get-tuple-element.290) | copy-start | bytes 196612
  490.4 3.3 collective-permute-start.8
  (62 other events, 225.1 us)
Sparse Core Ops, SparseCore 0:
  484.6 140.5 all-reduce.2
where the time goes:
time: 642 us; the launch traced here: 639 us
  waiting for transfers between devices  336 us (52%)
  matrix products  123 us (19%)
  local copies, waits for them, and re-layouts  75.9 us (12%)
  starting transfers between devices  50.3 us (8%)
  other arithmetic  39.1 us (6%)
  between operations  14.5 us (2%)
    ppermute x16, waiting for transfers between devices, passed_along_2(): lax.ppermute(value, axis, [(source, source + steps) for source in range(i...  201 us
    psum x1, waiting for transfers between devices, body(): lax.psum((down_map_gradient, up_map_gradient), ('section', 'ctx', 'dp'))  131 us
    ppermute x16, starting transfers between devices, passed_along_2(): lax.ppermute(value, axis, [(source, source + steps) for source in range(i...  50.3 us
    dot_general x16, matrix products, masked_scores(): jnp.einsum('trd,ld->trl', query_part, key_part, preferred_element_type=jn...  40.9 us
    dot_general x8, matrix products, group_backward(): jnp.einsum('trl,trd->ld', grad_scores, query_part, preferred_element_type...  31.1 us
    unnamed x52, local copies, waits for them, and re-layouts  26.1 us
    dot_general x8, matrix products, group_backward(): jnp.einsum('trl,trd->ld', weights_low, grad_part, preferred_element_type=...  24.3 us
    dot_general x8, matrix products, group_forward(): jnp.einsum('trl,ld->trd', weights, value_part, preferred_element_type=jnp...  18.2 us
  transfers between devices with their start and end apart: 19, of which 17 were waited for; matrix products, arithmetic and copies ran while one was open for 14% of the time, Pallas kernels for 0%

commit v1 on v0

--- a/solution.py
+++ b/solution.py
@@ -282,7 +282,7 @@
         value_gradient,
         adapter_up_maps,
     )
-    summed = lax.psum((down_map_gradient, up_map_gradient), ("section", "ctx", "dp"))
+    summed = lax.psum(lax.psum((down_map_gradient, up_map_gradient), "section"), ("ctx", "dp"))
     return (handed, summed[0], summed[1])
 
 

time: 642 us -> 683 us (1.064)
  waiting for transfers between devices: 336 us -> 377 us
    psum x1 -> x2, waiting for transfers between devices: 131 us -> 173 us  [the longest x1 148 us: body(): lax.psum(lax.psum((down_map_gradient, up_map_gradient), 'section'), ('ctx...]
  transfers between devices with their start and end apart: 19 -> 20, of which waited for: 17 -> 18; matrix products, arithmetic and copies ran while one was open for 14% -> 13% of each run, Pallas kernels for 0% -> 0%
where the time goes in v1:
time: 683 us; the launch traced here: 680 us
  waiting for transfers between devices  377 us (55%)
  matrix products  122 us (18%)
  local copies, waits for them, and re-layouts  75.9 us (11%)
  starting transfers between devices  50.4 us (7%)
  other arithmetic  39.1 us (6%)
  between operations  14.6 us (2%)
    ppermute x16, waiting for transfers between devices, passed_along_2(): lax.ppermute(value, axis, [(source, source + steps) for source in range(i...  201 us
    psum x1, waiting for transfers between devices, body(): lax.psum(lax.psum((down_map_gradient, up_map_gradient), 'section'), ('ctx...  148 us
    ppermute x16, starting transfers between devices, passed_along_2(): lax.ppermute(value, axis, [(source, source + steps) for source in range(i...  50.1 us
    dot_general x16, matrix products, masked_scores(): jnp.einsum('trd,ld->trl', query_part, key_part, preferred_element_type=jn...  41 us
    dot_general x8, matrix products, group_backward(): jnp.einsum('trl,trd->ld', grad_scores, query_part, preferred_element_type...  31 us
    unnamed x52, local copies, waits for them, and re-layouts  26.1 us
    psum x1, waiting for transfers between devices, body(): lax.psum((down_map_gradient, up_map_gradient), 'section')  25.2 us
    dot_general x8, matrix products, group_backward(): jnp.einsum('trl,trd->ld', weights_low, grad_part, preferred_element_type=...  24.3 us
  transfers between devices with their start and end apart: 20, of which 18 were waited for; matrix products, arithmetic and copies ran while one was open for 13% of the time, Pallas kernels for 0%

profile of v1, /device:TPU:0, one launch (start us, length us, event | category | flops | bytes accessed | tf_op | source)
XLA Modules:
  0.0 680.0 jit_solution(1407792490667414575)
XLA Ops:
  17.8 5.7 collective-permute-start
  28.1 6.9 %collective-permute-done = bf16[256,1024]{0,1:T(8,128)(2,1)} collective-permute-done((bf16[256,1024]{0,1:T(8,128)(2,1)S(1)}, bf16[256,1024]{0,1:T(8,128)(2,1)}, u32[]{:S(2)}, u32[]{:S(2)}) %collective-permute-start) | collective-permute-done | bytes 524320 | tf_op jit(solution)/shard_map/ppermute | solution.py:23
  35.0 5.3 collective-permute-start.1
  46.4 5.2 collective-permute-start.5
  51.6 6.0 collective-permute-done.1
  57.6 5.2 collective-permute-start.2
  68.8 5.2 collective-permute-start.6
  74.1 6.0 collective-permute-done.2
  80.1 4.4 collective-permute-start.3
  91.3 5.2 collective-permute-start.7
  96.5 6.1 collective-permute-done.3
  109.8 4.4 copy.48
  121.6 46.0 %while.26 = (s32[]{:T(128)}, bf16[8,256,2,128]{3,1,2,0:T(8,128)(2,1)}, f32[8,256,2]{1,2,0:T(2,128)}, bf16[8,256,2,128]{3,1,2,0:T(8,128)(2,1)}, bf16[8,1280,128]{...) while((s32[]{:T(128)}, ...), condition=%wide.region_8.9_spmd.clone, body=%wide.region_5.8_spmd.clone.sunk | while | flops 343145984 | bytes 9469813 | solution.py:245
  167.6 127.1 %while.27 = (s32[]{:T(128)}, f32[8,1280,128]{1,2,0:T(8,128)}, f32[8,1280,128]{1,2,0:T(8,128)}, bf16[8,256,2,128]{3,1,2,0:T(8,128)(2,1)}, bf16[8,1280,128]{2,1,0:...) while((s32[]{:T(128)}, f32[8,1280,128]{1,2,0:T(8,128)}, ...), condition=%wide.region_11.12_spmd.clone, body=%wide.region_9.11_spmd.clone.sunk | while | flops 678395392 | bytes 14472769 | solution.py:251
  301.3 24.9 %collective-permute-done.14 = f32[256,1024]{0,1:T(8,128)S(1)} collective-permute-done((f32[256,1024]{0,1:T(8,128)S(1)}, f32[256,1024]{0,1:T(8,128)S(1)}, u32[]{:S(2)}, u32[]{:S(2)}) %collective-permute-start.14) | collective-permute-done | bytes 1048608 | tf_op jit(solution)/shard_map/ppermute | solution.py:23
  327.6 21.0 %collective-permute-done.10 = f32[256,1024]{0,1:T(8,128)S(1)} collective-permute-done((f32[256,1024]{0,1:T(8,128)S(1)}, f32[256,1024]{0,1:T(8,128)S(1)}, u32[]{:S(2)}, u32[]{:S(2)}) %collective-permute-start.10) | collective-permute-done | bytes 1048608 | tf_op jit(solution)/shard_map/ppermute | solution.py:23
  350.1 21.0 %collective-permute-done.15 = f32[256,1024]{0,1:T(8,128)S(1)} collective-permute-done((f32[256,1024]{0,1:T(8,128)S(1)}, f32[256,1024]{0,1:T(8,128)S(1)}, u32[]{:S(2)}, u32[]{:S(2)}) %collective-permute-start.15) | collective-permute-done | bytes 1048608 | tf_op jit(solution)/shard_map/ppermute | solution.py:23
  372.6 21.0 %collective-permute-done.11 = f32[256,1024]{0,1:T(8,128)S(1)} collective-permute-done((f32[256,1024]{0,1:T(8,128)S(1)}, f32[256,1024]{0,1:T(8,128)S(1)}, u32[]{:S(2)}, u32[]{:S(2)}) %collective-permute-start.11) | collective-permute-done | bytes 1048608 | tf_op jit(solution)/shard_map/ppermute | solution.py:23
  395.0 21.0 %collective-permute-done.16 = f32[256,1024]{0,1:T(8,128)S(1)} collective-permute-done((f32[256,1024]{0,1:T(8,128)S(1)}, f32[256,1024]{0,1:T(8,128)S(1)}, u32[]{:S(2)}, u32[]{:S(2)}) %collective-permute-start.16) | collective-permute-done | bytes 1048608 | tf_op jit(solution)/shard_map/ppermute | solution.py:23
  417.5 21.0 %collective-permute-done.12 = f32[256,1024]{0,1:T(8,128)S(1)} collective-permute-done((f32[256,1024]{0,1:T(8,128)S(1)}, f32[256,1024]{0,1:T(8,128)S(1)}, u32[]{:S(2)}, u32[]{:S(2)}) %collective-permute-start.12) | collective-permute-done | bytes 1048608 | tf_op jit(solution)/shard_map/ppermute | solution.py:23
  440.0 21.0 %collective-permute-done.17 = f32[256,1024]{0,1:T(8,128)S(1)} collective-permute-done((f32[256,1024]{0,1:T(8,128)S(1)}, f32[256,1024]{0,1:T(8,128)S(1)}, u32[]{:S(2)}, u32[]{:S(2)}) %collective-permute-start.17) | collective-permute-done | bytes 1048608 | tf_op jit(solution)/shard_map/ppermute | solution.py:23
  461.7 18.9 %collective-permute-done.13 = f32[256,1024]{0,1:T(8,128)S(1)} collective-permute-done((f32[256,1024]{0,1:T(8,128)S(1)}, f32[256,1024]{0,1:T(8,128)S(1)}, u32[]{:S(2)}, u32[]{:S(2)}) %collective-permute-start.13) | collective-permute-done | bytes 1048608 | tf_op jit(solution)/shard_map/ppermute | solution.py:23
  484.6 25.2 %all-reduce.7.cloned.1.call-done = (f32[5376,2,4,16]{0,3,2,1:T(8,128)}, f32[2,4,16,1024]{3,2,1,0:T(8,128)}) async-done(((f32[5376,2,4,16]{0,3,2,1:T(8,128)}, f32[2,4,16,1024]{3,2,1,0:T(8,128)}), (f32[5376,2,4,16]{0,3,2,1:T(8,128)}, f32[2,4,16,1024]{3,2,1,0:T(8,128)})) %all-reduce.7.cloned.1.call-update) | async-done | bytes 3276816 | tf_op jit(solution)/shard_map/psum | solution.py:285
  518.7 147.8 %all-reduce.5.cloned.1.call-done = (f32[5376,2,4,16]{0,3,2,1:T(8,128)}, f32[2,4,16,1024]{3,2,1,0:T(8,128)}) async-done(((f32[5376,2,4,16]{0,3,2,1:T(8,128)}, f32[2,4,16,1024]{3,2,1,0:T(8,128)}), (f32[5376,2,4,16]{0,3,2,1:T(8,128)}, f32[2,4,16,1024]{3,2,1,0:T(8,128)})) %all-reduce.5.cloned.1.call-update) | async-done | bytes 3276816 | tf_op jit(solution)/shard_map/psum | solution.py:285
  (346 shorter events, 256.2 us)
Async XLA Ops:
  7.2 502.6 %all-reduce.7.cloned.1.call-start = ((), (), s32[]{:S(2)}) async-start(), calls=%async_computation.1 | async-start | bytes 6553600 | tf_op jit(solution)/shard_map/psum | solution.py:285
  17.8 17.2 %collective-permute-start = (bf16[256,1024]{0,1:T(8,128)(2,1)S(1)}, bf16[256,1024]{0,1:T(8,128)(2,1)}, u32[]{:S(2)}, u32[]{:S(2)}) collective-permute-start(bf16[256,1024]{0,1:T(8,128)(2,1)S(1)} %bitcast.243), channel_id=1, source_target_pairs={{0,2},{2,4},{4,6},{6,8},{8,10},{10,12},{12,14},{1,3},{3,5},{5,7},{... | collective-permute-start | bytes 1572872 | tf_op jit(solution)/shard_map/ppermute | solution.py:23
  24.7 21.7 %collective-permute-start.4 = (bf16[256,1024]{1,0:T(8,128)(2,1)}, bf16[256,1024]{1,0:T(8,128)(2,1)}, u32[]{:S(2)}, u32[]{:S(2)}) collective-permute-start(bf16[256,1024]{1,0:T(8,128)(2,1)} %fusion.59), channel_id=1, source_target_pairs={{0,2},{2,4},{4,6},{6,8},{8,10},{10,12},{12,14},{1,3},{3,5},{5,7},{... | collective-permute-start | bytes 1572872 | tf_op jit(solution)/shard_map/ppermute | solution.py:23
  35.0 22.6 %collective-permute-start.1 = (bf16[256,1024]{0,1:T(8,128)(2,1)}, bf16[256,1024]{0,1:T(8,128)(2,1)}, u32[]{:S(2)}, u32[]{:S(2)}) collective-permute-start(bf16[256,1024]{0,1:T(8,128)(2,1)} %collective-permute-done), channel_id=1, source_target_pairs={{0,2},{2,4},{4,6},{6,8},{8,10},{10,12},{12,14},{1,3},{3,5},{5,7},{... | collective-permute-start | bytes 1572872 | tf_op jit(solution)/shard_map/ppermute | solution.py:23
  42.6 125.1 %collective-permute-start.9 = (bf16[1,256,2048]{1,2,0:T(8,128)(2,1)}, bf16[1,256,2048]{1,2,0:T(8,128)(2,1)}, u32[]{:S(2)}, u32[]{:S(2)}) collective-permute-start(bf16[1,256,2048]{1,2,0:T(8,128)(2,1)} %copy.50), channel_id=1, source_target_pairs={{0,16},{16,0},{1,17},{17,1},{2,18},{18,2},{3,19},{19,3},{4,20},{20... | collective-permute-start | bytes 3145736 | tf_op jit(solution)/shard_map/ppermute | solution.py:17
  46.4 22.5 %collective-permute-start.5 = (bf16[256,1024]{1,0:T(8,128)(2,1)}, bf16[256,1024]{1,0:T(8,128)(2,1)}, u32[]{:S(2)}, u32[]{:S(2)}) collective-permute-start(bf16[256,1024]{1,0:T(8,128)(2,1)} %collective-permute-done.4), channel_id=1, source_target_pairs={{0,2},{2,4},{4,6},{6,8},{8,10},{10,12},{12,14},{1,3},{3,5},{5,7},{... | collective-permute-start | bytes 1572872 | tf_op jit(solution)/shard_map/ppermute | solution.py:23
  57.6 22.5 %collective-permute-start.2 = (bf16[256,1024]{0,1:T(8,128)(2,1)}, bf16[256,1024]{0,1:T(8,128)(2,1)}, u32[]{:S(2)}, u32[]{:S(2)}) collective-permute-start(bf16[256,1024]{0,1:T(8,128)(2,1)} %collective-permute-done.1), channel_id=1, source_target_pairs={{0,2},{2,4},{4,6},{6,8},{8,10},{10,12},{12,14},{1,3},{3,5},{5,7},{... | collective-permute-start | bytes 1572872 | tf_op jit(solution)/shard_map/ppermute | solution.py:23
  66.9 17.5 %copy-start.1 = (f32[256,64]{1,0:T(8,128)S(1)}, f32[256,64]{1,0:T(8,128)}, u32[]{:S(2)}) copy-start(f32[256,64]{1,0:T(8,128)} %copy.41) | copy-start | bytes 196612
  67.0 17.5 %copy-start.2 = (f32[256,64]{1,0:T(8,128)S(1)}, f32[256,64]{1,0:T(8,128)}, u32[]{:S(2)}) copy-start(f32[256,64]{1,0:T(8,128)} %copy.43) | copy-start | bytes 196612
  68.8 22.5 %collective-permute-start.6 = (bf16[256,1024]{1,0:T(8,128)(2,1)}, bf16[256,1024]{1,0:T(8,128)(2,1)}, u32[]{:S(2)}, u32[]{:S(2)}) collective-permute-start(bf16[256,1024]{1,0:T(8,128)(2,1)} %collective-permute-done.5), channel_id=1, source_target_pairs={{0,2},{2,4},{4,6},{6,8},{8,10},{10,12},{12,14},{1,3},{3,5},{5,7},{... | collective-permute-start | bytes 1572872 | tf_op jit(solution)/shard_map/ppermute | solution.py:23
  80.1 22.5 %collective-permute-start.3 = (bf16[256,1024]{0,1:T(8,128)(2,1)}, bf16[256,1024]{0,1:T(8,128)(2,1)S(1)}, u32[]{:S(2)}, u32[]{:S(2)}) collective-permute-start(bf16[256,1024]{0,1:T(8,128)(2,1)} %collective-permute-done.2), channel_id=1, source_target_pairs={{0,2},{2,4},{4,6},{6,8},{8,10},{10,12},{12,14},{1,3},{3,5},{5,7},{... | collective-permute-start | bytes 1572872 | tf_op jit(solution)/shard_map/ppermute | solution.py:23
  91.3 22.9 %collective-permute-start.7 = (bf16[256,1024]{1,0:T(8,128)(2,1)}, bf16[256,1024]{1,0:T(8,128)(2,1)}, u32[]{:S(2)}, u32[]{:S(2)}) collective-permute-start(bf16[256,1024]{1,0:T(8,128)(2,1)} %collective-permute-done.6), channel_id=1, source_target_pairs={{0,2},{2,4},{4,6},{6,8},{8,10},{10,12},{12,14},{1,3},{3,5},{5,7},{... | collective-permute-start | bytes 1572872 | tf_op jit(solution)/shard_map/ppermute | solution.py:23
  297.8 28.4 %collective-permute-start.14 = (f32[256,1024]{0,1:T(8,128)S(1)}, f32[256,1024]{0,1:T(8,128)S(1)}, u32[]{:S(2)}, u32[]{:S(2)}) collective-permute-start(f32[256,1024]{0,1:T(8,128)S(1)} %bitcast.238), channel_id=1, source_target_pairs={{2,0},{4,2},{6,4},{8,6},{10,8},{12,10},{14,12},{3,1},{5,3},{7,5},{... | collective-permute-start | bytes 3145736 | tf_op jit(solution)/shard_map/ppermute | solution.py:23
  300.0 48.7 %collective-permute-start.10 = (f32[256,1024]{0,1:T(8,128)S(1)}, f32[256,1024]{0,1:T(8,128)S(1)}, u32[]{:S(2)}, u32[]{:S(2)}) collective-permute-start(f32[256,1024]{0,1:T(8,128)S(1)} %bitcast.239), channel_id=1, source_target_pairs={{2,0},{4,2},{6,4},{8,6},{10,8},{12,10},{14,12},{3,1},{5,3},{7,5},{... | collective-permute-start | bytes 3145736 | tf_op jit(solution)/shard_map/ppermute | solution.py:23
  326.3 44.8 %collective-permute-start.15 = (f32[256,1024]{0,1:T(8,128)S(1)}, f32[256,1024]{0,1:T(8,128)S(1)}, u32[]{:S(2)}, u32[]{:S(2)}) collective-permute-start(f32[256,1024]{0,1:T(8,128)S(1)} %bitcast_add_fusion.3), channel_id=1, source_target_pairs={{2,0},{4,2},{6,4},{8,6},{10,8},{12,10},{14,12},{3,1},{5,3},{7,5},{... | collective-permute-start | bytes 3145736 | tf_op jit(solution)/shard_map/ppermute | solution.py:23
  348.8 44.8 %collective-permute-start.11 = (f32[256,1024]{0,1:T(8,128)S(1)}, f32[256,1024]{0,1:T(8,128)S(1)}, u32[]{:S(2)}, u32[]{:S(2)}) collective-permute-start(f32[256,1024]{0,1:T(8,128)S(1)} %bitcast_add_fusion.7), channel_id=1, source_target_pairs={{2,0},{4,2},{6,4},{8,6},{10,8},{12,10},{14,12},{3,1},{5,3},{7,5},{... | collective-permute-start | bytes 3145736 | tf_op jit(solution)/shard_map/ppermute | solution.py:23
  371.3 44.8 %collective-permute-start.16 = (f32[256,1024]{0,1:T(8,128)S(1)}, f32[256,1024]{0,1:T(8,128)S(1)}, u32[]{:S(2)}, u32[]{:S(2)}) collective-permute-start(f32[256,1024]{0,1:T(8,128)S(1)} %bitcast_add_fusion.2), channel_id=1, source_target_pairs={{2,0},{4,2},{6,4},{8,6},{10,8},{12,10},{14,12},{3,1},{5,3},{7,5},{... | collective-permute-start | bytes 3145736 | tf_op jit(solution)/shard_map/ppermute | solution.py:23
  393.7 44.8 %collective-permute-start.12 = (f32[256,1024]{0,1:T(8,128)S(1)}, f32[256,1024]{0,1:T(8,128)S(1)}, u32[]{:S(2)}, u32[]{:S(2)}) collective-permute-start(f32[256,1024]{0,1:T(8,128)S(1)} %bitcast_add_fusion.6), channel_id=1, source_target_pairs={{2,0},{4,2},{6,4},{8,6},{10,8},{12,10},{14,12},{3,1},{5,3},{7,5},{... | collective-permute-start | bytes 3145736 | tf_op jit(solution)/shard_map/ppermute | solution.py:23
  416.1 23.9 %copy-start.6 = (bf16[2,4,16,1024]{3,2,1,0:T(8,128)(2,1)S(1)}, bf16[2,4,16,1024]{3,2,1,0:T(8,128)(2,1)}, u32[]{:S(2)}) copy-start(bf16[2,4,16,1024]{3,2,1,0:T(8,128)(2,1)} %param.21) | copy-start | bytes 786436
  416.2 44.8 %collective-permute-start.17 = (f32[256,1024]{0,1:T(8,128)S(1)}, f32[256,1024]{0,1:T(8,128)S(1)}, u32[]{:S(2)}, u32[]{:S(2)}) collective-permute-start(f32[256,1024]{0,1:T(8,128)S(1)} %bitcast_add_fusion.1), channel_id=1, source_target_pairs={{2,0},{4,2},{6,4},{8,6},{10,8},{12,10},{14,12},{3,1},{5,3},{7,5},{... | collective-permute-start | bytes 3145736 | tf_op jit(solution)/shard_map/ppermute | solution.py:23
  438.7 42.0 %collective-permute-start.13 = (f32[256,1024]{0,1:T(8,128)S(1)}, f32[256,1024]{0,1:T(8,128)S(1)}, u32[]{:S(2)}, u32[]{:S(2)}) collective-permute-start(f32[256,1024]{0,1:T(8,128)S(1)} %bitcast_add_fusion.5), channel_id=1, source_target_pairs={{2,0},{4,2},{6,4},{8,6},{10,8},{12,10},{14,12},{3,1},{5,3},{7,5},{... | collective-permute-start | bytes 3145736 | tf_op jit(solution)/shard_map/ppermute | solution.py:23
  461.2 19.6 %copy-start.7 = (f32[256,64]{0,1:T(8,128)S(1)}, f32[256,64]{0,1:T(8,128)}, u32[]{:S(2)}) copy-start(f32[256,64]{0,1:T(8,128)} %get-tuple-element.292) | copy-start | bytes 196612
  484.5 182.0 %all-reduce.5.cloned.1.call-start = ((), (), s32[]{:S(2)}) async-start(), calls=%async_computation | async-start | bytes 6553600 | tf_op jit(solution)/shard_map/psum | solution.py:285
  515.7 3.0 collective-permute-start.8
  (63 other events, 233.3 us)
Sparse Core Ops, SparseCore 0:
  484.6 25.0 all-reduce.6
  515.4 151.0 all-reduce.4
